TPU v7x, 256 devices: a whole 4x4x8 slice. The times are simulated.
256 devices in a mesh: tok: 64 (over z, y, core), unit: 4 (over x).
Axes of the slice: x: 4, y: 4, z: 8, core: 2. Of those that a mesh axis runs over, the one named last changes fastest.
Arguments:
- act_a: bfloat16 [131072, 3072], P('tok', 'unit'), may hold values from -4000 to 4000
- act_b: bfloat16 [131072, 3072], P(('tok', 'unit')), may hold values from -4000 to 4000
Outputs:
- correlation: float32 [3072, 3072], P('tok', 'unit')
All inputs are finite; a program needn't handle non-finite values.
Results may differ from a plain program's by a relative error of at most 0.0003.
Values may be sent and summed in bfloat16 or wider, within the bound.
No kernel may reach another device: no remote copies, remote signals or barrier semaphores. Data moves between devices by JAX's collectives and lax.ppermute only.
A program may use at most 128 MiB of HBM per device.

v0:
```python
import functools
import jax
import jax.numpy as jnp
from jax import lax
from jax.sharding import Mesh
from jax.sharding import PartitionSpec as P

TOK = ("tok_0", "tok_1", "tok_2")
TOK_UNIT = ("tok_0", "tok_1", "tok_2", "unit")


def by_axis(array, axes):
    return functools.reduce(lax.psum, axes, array)


def contract_tokens(left, right):
    return lax.dot_general(
        left, right, (((0,), (0,)), ((), ())), preferred_element_type=jnp.float32
    )


def per_device(act_a, act_b):
    token_rows, own_units = act_a.shape
    units = act_b.shape[1]
    groups = lax.axis_size(TOK)
    band = units // groups
    total_tokens = token_rows * groups
    wide_a = act_a.astype(jnp.float32)
    first_total = jnp.sum(wide_a, axis=0)
    first_square = jnp.sum(wide_a * wide_a, axis=0)
    piece = lax.all_gather(act_b, "unit", axis=0, tiled=True)
    product = contract_tokens(piece, act_a)
    wide_piece = piece.astype(jnp.float32)
    second_total = jnp.sum(wide_piece, axis=0)
    second_square = jnp.sum(wide_piece * wide_piece, axis=0)
    product, second_total, second_square = (product, second_total, second_square)
    shares = lax.psum_scatter(product, TOK, scatter_dimension=0, tiled=True)
    first_all, first_square_all, second_all, second_square_all = (
        by_axis(first_total, TOK),
        by_axis(first_square, TOK),
        by_axis(second_total, TOK),
        by_axis(second_square, TOK),
    )
    offset = lax.axis_index(TOK) * band
    second_own = lax.dynamic_slice_in_dim(second_all, offset, band, 0)
    second_square_own = lax.dynamic_slice_in_dim(second_square_all, offset, band, 0)
    mean_a = first_all / total_tokens
    var_a = first_square_all / total_tokens - mean_a * mean_a
    mean_b = second_own / total_tokens
    var_b = second_square_own / total_tokens - mean_b * mean_b
    centered = shares / total_tokens - mean_b[:, None] * mean_a[None, :]
    return centered / (jnp.sqrt(var_b + 1e-05)[:, None] * jnp.sqrt(var_a + 1e-05)[None, :])


def solution(mesh):
    torus = Mesh(
        mesh.devices.reshape(8, 4, 2, mesh.shape["unit"]), ("tok_0", "tok_1", "tok_2", "unit")
    )
    placed = (P(TOK, "unit"), P(TOK_UNIT, None))
    return jax.shard_map(
        per_device, mesh=torus, in_specs=placed, out_specs=P(TOK, "unit"), check_vma=False
    )
```

profile of v0, /device:TPU:2, one launch (start us, length us, event | category | flops | bytes accessed | tf_op | source)
XLA Modules:
  0.0 314.8 jit_solution(7686966952882575535)
XLA Ops:
  6.5 0.0 all-gather.2.cloned.1.call-start
  6.5 0.7 all-gather.2.cloned.1.call-update
  7.3 0.0 reduce-scatter.2.cloned.1.call-start
  7.3 125.9 %all-gather.2.cloned.1.call-done = bf16[2048,3072]{1,0:T(8,128)(2,1)} async-done(((bf16[512,3072]{1,0:T(8,128)(2,1)}), bf16[2048,3072]{1,0:T(8,128)(2,1)}) %all-gather.2.cloned.1.call-update) | async-done | bytes 12582928 | tf_op jit(solution)/shard_map/all_gather | solution.py:31
  133.2 16.3 %fusion.2 = f32[3072,768]{1,0:T(8,128)} fusion(bf16[2048,3072]{1,0:T(8,128)(2,1)} %all-gather.2.cloned.1.call-done, bf16[2048,768]{1,0:T(8,128)(2,1)} %param.2), kind=kOutput, calls=%fused_computation.11 | convolution fusion | flops 9663676416 | bytes 25165824 | tf_op jit(solution)/shard_map/dot_general | solution.py:17
  149.5 0.0 copy-start
  149.5 0.0 reduce-scatter.2.cloned.1.call-update
  149.5 1.9 copy-done
  151.4 0.9 convert_reduce_fusion.1
  152.2 8.0 %convert_reduce_fusion = (f32[3072]{0:T(1024)S(1)}, f32[3072]{0:T(1024)S(1)}) fusion(bf16[2048,3072]{1,0:T(8,128)(2,1)} %all-gather.2.cloned.1.call-done), kind=kLoop, calls=%fused_computation.1 | loop fusion | flops 25159680 | bytes 12607488 | tf_op jit(solution)/shard_map/reduce_sum | solution.py:34
  160.2 30.2 %all-reduce = (f32[768]{0:T(1024)S(1)}, f32[768]{0:T(1024)S(1)}, f32[3072]{0:T(1024)S(1)}, f32[3072]{0:T(1024)S(1)}) all-reduce(f32[768]{0:T(1024)S(1)} %get-tuple-element.8, f32[768]{0:T(1024)S(1)} %get-tuple-element.7, f32[3072]{0:T(1024)S(1)} %get-tuple-element.6, ...), channel_id=1, replica_groups=mesh['tok_0'=8,'tok_1'=4,'tok_2'=2,'unit'=4] {'tok_0'}, use_global_device_ids=true, to_apply=%region_14.0 | all-reduce | flops 7680 | bytes 61440 | tf_op jit(solution)/shard_map/psum | solution.py:13
  190.4 17.1 %all-reduce.1 = (f32[768]{0:T(1024)S(1)}, f32[768]{0:T(1024)S(1)}, f32[3072]{0:T(1024)S(1)}, f32[3072]{0:T(1024)S(1)}) all-reduce(f32[768]{0:T(1024)S(1)} %get-tuple-element.9, f32[768]{0:T(1024)S(1)} %get-tuple-element.10, f32[3072]{0:T(1024)S(1)} %get-tuple-element.11, ...), channel_id=1, replica_groups=mesh['tok_0'=8,'tok_1'=4,'tok_2'=2,'unit'=4] {'tok_1'}, use_global_device_ids=true, to_apply=%region_15.0 | all-reduce | flops 7680 | bytes 61440 | tf_op jit(solution)/shard_map/psum | solution.py:13
  207.5 3.4 %all-reduce.2 = (f32[768]{0:T(1024)S(1)}, f32[768]{0:T(1024)S(1)}, f32[3072]{0:T(1024)S(1)}, f32[3072]{0:T(1024)S(1)}) all-reduce(f32[768]{0:T(1024)S(1)} %get-tuple-element.13, f32[768]{0:T(1024)S(1)} %get-tuple-element.14, f32[3072]{0:T(1024)S(1)} %get-tuple-element.15, ...), channel_id=1, replica_groups=mesh['tok_0'=8,'tok_1'=4,'tok_2'=2,'unit'=4] {'tok_2'}, use_global_device_ids=true, to_apply=%region_16.0 | all-reduce | flops 7680 | bytes 61440 | tf_op jit(solution)/shard_map/psum | solution.py:13
  210.9 0.1 dynamic-slice_multiply_fusion
  211.0 95.2 %reduce-scatter.2.cloned.1.call-done = f32[48,768]{1,0:T(8,128)} async-done(((f32[3072,768]{1,0:T(8,128)}), f32[48,768]{1,0:T(8,128)}) %reduce-scatter.2.cloned.1.call-update) | async-done | bytes 147472 | tf_op jit(solution)/shard_map/reduce_scatter | solution.py:37
  306.3 1.7 multiply_divide_fusion
  (1 shorter events, 0.0 us)
Async XLA Ops:
  6.5 126.7 %all-gather.2.cloned.1.call-start = ((), (), s32[]{:S(2)}) async-start(), calls=%async_computation.1 | async-start | bytes 15728640 | tf_op jit(solution)/shard_map/all_gather | solution.py:31
  7.3 299.0 %reduce-scatter.2.cloned.1.call-start = ((), (), s32[]{:S(2)}) async-start(), calls=%async_computation.2 | async-start | bytes 9584640 | tf_op jit(solution)/shard_map/reduce_scatter | solution.py:37
  149.5 1.9 copy-start
Sparse Core Ops, SparseCore 0:
  9.1 124.0 all-gather.1
  149.6 156.6 reduce-scatter.1
where the time goes:
time: 315 us
  waiting for transfers between devices  222 us (70%)
  blocking collectives  50.7 us (16%)
  matrix products  16.3 us (5%)
  between operations  13.4 us (4%)
  other arithmetic  10.6 us (3%)
    all_gather x1, waiting for transfers between devices, per_device(): piece = lax.all_gather(act_b, 'unit', axis=0, tiled=True)  126 us
    reduce_scatter x1, waiting for transfers between devices, per_device(): shares = lax.psum_scatter(product, TOK, scatter_dimension=0, tiled=True)  95.2 us
    psum x3, blocking collectives, by_axis(): return functools.reduce(lax.psum, axes, array)  50.7 us
    dot_general x1, matrix products, contract_tokens(): lax.dot_general(left, right, (((0,), (0,)), ((), ())), preferred_element_...  16.3 us
    reduce_sum x1, other arithmetic, per_device(): second_total = jnp.sum(wide_piece, axis=0)  7.99 us
  transfers between devices with their start and end apart: 2, of which 2 were waited for; matrix products, arithmetic and copies ran while one was open for 3% of the time, Pallas kernels for 0%

commit v1 on v0

--- a/solution.py
+++ b/solution.py
@@ -7,6 +7,27 @@
 
 TOK = ("tok_0", "tok_1", "tok_2")
 TOK_UNIT = ("tok_0", "tok_1", "tok_2", "unit")
+
+
+def ring_gather(value, axis, dim):
+    count, index, rows = (lax.axis_size(axis), lax.axis_index(axis), value.shape[dim])
+    forward = [(i, (i + 1) % count) for i in range(count)]
+    behind = [(i, (i - 1) % count) for i in range(count)]
+    out = jnp.zeros((*value.shape[:dim], count * rows, *value.shape[dim + 1 :]), value.dtype)
+    out = lax.dynamic_update_slice_in_dim(out, value, index * rows, axis=dim)
+    from_left = from_right = value
+    middle = count // 2
+    for step in range(1, middle + 1):
+        from_left = lax.ppermute(from_left, axis, forward)
+        out = lax.dynamic_update_slice_in_dim(
+            out, from_left, (index - step) % count * rows, axis=dim
+        )
+        if step < count - middle:
+            from_right = lax.ppermute(from_right, axis, behind)
+            out = lax.dynamic_update_slice_in_dim(
+                out, from_right, (index + step) % count * rows, axis=dim
+            )
+    return out
 
 
 def by_axis(array, axes):
@@ -28,7 +49,7 @@
     wide_a = act_a.astype(jnp.float32)
     first_total = jnp.sum(wide_a, axis=0)
     first_square = jnp.sum(wide_a * wide_a, axis=0)
-    piece = lax.all_gather(act_b, "unit", axis=0, tiled=True)
+    piece = ring_gather(act_b, "unit", 0)
     product = contract_tokens(piece, act_a)
     wide_piece = piece.astype(jnp.float32)
     second_total = jnp.sum(wide_piece, axis=0)

time: 315 us -> 333 us (1.057)
  local copies, waits for them, and re-layouts: 1.85 us -> 19.5 us
  waiting for transfers between devices: 222 us -> 216 us
  starting transfers between devices: 0.04 us -> 3.74 us
    all_gather x1 -> x0, waiting for transfers between devices: 126 us -> none  [per_device(): piece = lax.all_gather(act_b, 'unit', axis=0, tiled=True)]
    ppermute x0 -> x3, waiting for transfers between devices: none -> 120 us  [the longest x2 120 us: ring_gather(): from_left = lax.ppermute(from_left, axis, forward)]
    dynamic_update_slice x0 -> x4, local copies, waits for them, and re-layouts: none -> 13.3 us  [the longest x2 7.65 us: ring_gather(): lax.dynamic_update_slice_in_dim(out, from_left, (index - step) % count *...]
    broadcast_in_dim x0 -> x1, local copies, waits for them, and re-layouts: none -> 6.16 us  [ring_gather(): jnp.zeros((*value.shape[:dim], count * rows, *value.shape[dim + 1:]), val...]
    ppermute x0 -> x3, starting transfers between devices: none -> 3.74 us  [the longest x2 2.98 us: ring_gather(): from_left = lax.ppermute(from_left, axis, forward)]
  transfers between devices with their start and end apart: 2 -> 4, of which waited for: 2 -> 3; matrix products, arithmetic and copies ran while one was open for 3% -> 7% of each run, Pallas kernels for 0% -> 0%
where the time goes in v1:
time: 333 us; the launch traced here: 332 us
  waiting for transfers between devices  216 us (65%)
  blocking collectives  53.8 us (16%)
  local copies, waits for them, and re-layouts  19.5 us (6%)
  matrix products  15.4 us (5%)
  between operations  13.4 us (4%)
  other arithmetic  10.6 us (3%)
  starting transfers between devices  3.74 us (1%)
    ppermute x2, waiting for transfers between devices, ring_gather(): from_left = lax.ppermute(from_left, axis, forward)  120 us
    reduce_scatter x1, waiting for transfers between devices, per_device(): shares = lax.psum_scatter(product, TOK, scatter_dimension=0, tiled=True)  96.2 us
    psum x3, blocking collectives, by_axis(): return functools.reduce(lax.psum, axes, array)  53.8 us
    dot_general x1, matrix products, contract_tokens(): lax.dot_general(left, right, (((0,), (0,)), ((), ())), preferred_element_...  15.4 us
    reduce_sum x1, other arithmetic, per_device(): second_total = jnp.sum(wide_piece, axis=0)  8 us
    dynamic_update_slice x2, local copies, waits for them, and re-layouts, ring_gather(): lax.dynamic_update_slice_in_dim(out, from_left, (index - step) % count *...  7.65 us
  transfers between devices with their start and end apart: 4, of which 3 were waited for; matrix products, arithmetic and copies ran while one was open for 7% of the time, Pallas kernels for 0%

profile of v1, /device:TPU:2, one launch (start us, length us, event | category | flops | bytes accessed | tf_op | source)
XLA Modules:
  0.0 332.4 jit_solution(5492814164894126894)
XLA Ops:
  6.5 0.0 copy-start
  6.5 0.0 reduce-scatter.2.cloned.1.call-start
  6.5 1.5 collective-permute-start
  8.0 0.8 collective-permute-start.1
  8.8 67.9 %collective-permute-done = bf16[512,3072]{1,0:T(8,128)(2,1)} collective-permute-done((bf16[512,3072]{1,0:T(8,128)(2,1)}, bf16[512,3072]{1,0:T(8,128)(2,1)}, u32[]{:S(2)}, u32[]{:S(2)}) %collective-permute-start) | collective-permute-done | bytes 3145760 | tf_op jit(solution)/shard_map/ppermute | solution.py:21
  76.7 1.5 collective-permute-start.2
  78.2 6.2 %broadcast_in_dim.2 = bf16[2048,3072]{1,0:T(8,128)(2,1)} broadcast(bf16[]{:T(256)} %constant.52.clone.1), dimensions={} | broadcast | bytes 12582914 | tf_op jit(solution)/shard_map/broadcast_in_dim | solution.py:16
  84.4 0.0 copy-done
  84.4 0.0 copy-start.1
  84.4 1.9 constant_dynamic-update-slice_fusion.3
  86.3 3.9 %constant_dynamic-update-slice_fusion.2 = bf16[2048,3072]{1,0:T(8,128)(2,1)} fusion(bf16[2048,3072]{1,0:T(8,128)(2,1)} %constant_dynamic-update-slice_fusion.3, bf16[512,3072]{1,0:T(8,128)(2,1)} %collective-permute-done, s32[]{:T(128)S(6)} %select_n.33), kind=kLoop, calls=%fused_computation.11 | loop fusion | bytes 6291460 | tf_op jit(solution)/shard_map/dynamic_update_slice | solution.py:22
  90.2 0.0 collective-permute-done.1
  90.2 3.8 %constant_dynamic-update-slice_fusion.1 = bf16[2048,3072]{1,0:T(8,128)(2,1)} fusion(bf16[2048,3072]{1,0:T(8,128)(2,1)} %constant_dynamic-update-slice_fusion.2, bf16[512,3072]{1,0:T(8,128)(2,1)} %collective-permute-done.1, s32[]{:T(128)S(6)} %select_n.35), kind=kLoop, calls=%fused_computation.10 | loop fusion | bytes 6291460 | tf_op jit(solution)/shard_map/dynamic_update_slice | solution.py:27
  94.0 51.7 %collective-permute-done.2 = bf16[512,3072]{1,0:T(8,128)(2,1)} collective-permute-done((bf16[512,3072]{1,0:T(8,128)(2,1)}, bf16[512,3072]{1,0:T(8,128)(2,1)}, u32[]{:S(2)}, u32[]{:S(2)}) %collective-permute-start.2) | collective-permute-done | bytes 3145760 | tf_op jit(solution)/shard_map/ppermute | solution.py:21
  145.7 3.7 %constant_dynamic-update-slice_fusion = bf16[2048,3072]{1,0:T(8,128)(2,1)} fusion(bf16[2048,3072]{1,0:T(8,128)(2,1)} %constant_dynamic-update-slice_fusion.1, bf16[512,3072]{1,0:T(8,128)(2,1)} %collective-permute-done.2, s32[]{:T(128)S(6)} %select_n.37), kind=kLoop, calls=%fused_computation.9 | loop fusion | bytes 6291460 | tf_op jit(solution)/shard_map/dynamic_update_slice | solution.py:22
  149.4 0.0 copy-done.1
  149.4 0.0 copy-start.2
  149.4 15.4 %fusion.2 = f32[3072,768]{1,0:T(8,128)} fusion(bf16[2048,3072]{1,0:T(8,128)(2,1)} %constant_dynamic-update-slice_fusion, bf16[2048,768]{1,0:T(8,128)(2,1)S(1)} %copy-done.1), kind=kOutput, calls=%fused_computation.15 | convolution fusion | flops 9663676416 | bytes 25165824 | tf_op jit(solution)/shard_map/dot_general | solution.py:38
  164.9 0.0 reduce-scatter.2.cloned.1.call-update
  164.9 0.0 copy-done.2
  164.9 0.9 convert_reduce_fusion.1
  165.8 8.0 %convert_reduce_fusion = (f32[3072]{0:T(1024)S(1)}, f32[3072]{0:T(1024)S(1)}) fusion(bf16[2048,3072]{1,0:T(8,128)(2,1)} %constant_dynamic-update-slice_fusion), kind=kLoop, calls=%fused_computation.1 | loop fusion | flops 25159680 | bytes 12607488 | tf_op jit(solution)/shard_map/reduce_sum | solution.py:55
  173.8 33.1 %all-reduce = (f32[768]{0:T(1024)S(1)}, f32[768]{0:T(1024)S(1)}, f32[3072]{0:T(1024)S(1)}, f32[3072]{0:T(1024)S(1)}) all-reduce(f32[768]{0:T(1024)S(1)} %get-tuple-element.8, f32[768]{0:T(1024)S(1)} %get-tuple-element.7, f32[3072]{0:T(1024)S(1)} %get-tuple-element.6, ...), channel_id=1, replica_groups=mesh['tok_0'=8,'tok_1'=4,'tok_2'=2,'unit'=4] {'tok_0'}, use_global_device_ids=true, to_apply=%region_14.15 | all-reduce | flops 7680 | bytes 61440 | tf_op jit(solution)/shard_map/psum | solution.py:34
  206.8 17.3 %all-reduce.1 = (f32[768]{0:T(1024)S(1)}, f32[768]{0:T(1024)S(1)}, f32[3072]{0:T(1024)S(1)}, f32[3072]{0:T(1024)S(1)}) all-reduce(f32[768]{0:T(1024)S(1)} %get-tuple-element.9, f32[768]{0:T(1024)S(1)} %get-tuple-element.10, f32[3072]{0:T(1024)S(1)} %get-tuple-element.11, ...), channel_id=1, replica_groups=mesh['tok_0'=8,'tok_1'=4,'tok_2'=2,'unit'=4] {'tok_1'}, use_global_device_ids=true, to_apply=%region_15.16 | all-reduce | flops 7680 | bytes 61440 | tf_op jit(solution)/shard_map/psum | solution.py:34
  224.1 3.4 %all-reduce.2 = (f32[768]{0:T(1024)S(1)}, f32[768]{0:T(1024)S(1)}, f32[3072]{0:T(1024)S(1)}, f32[3072]{0:T(1024)S(1)}) all-reduce(f32[768]{0:T(1024)S(1)} %get-tuple-element.13, f32[768]{0:T(1024)S(1)} %get-tuple-element.14, f32[3072]{0:T(1024)S(1)} %get-tuple-element.15, ...), channel_id=1, replica_groups=mesh['tok_0'=8,'tok_1'=4,'tok_2'=2,'unit'=4] {'tok_2'}, use_global_device_ids=true, to_apply=%region_16.17 | all-reduce | flops 7680 | bytes 61440 | tf_op jit(solution)/shard_map/psum | solution.py:34
  227.6 0.1 dynamic-slice_multiply_fusion
  227.7 96.2 %reduce-scatter.2.cloned.1.call-done = f32[48,768]{1,0:T(8,128)} async-done(((f32[3072,768]{1,0:T(8,128)}), f32[48,768]{1,0:T(8,128)}) %reduce-scatter.2.cloned.1.call-update) | async-done | bytes 147472 | tf_op jit(solution)/shard_map/reduce_scatter | solution.py:58
  323.9 1.7 multiply_divide_fusion
  (1 shorter events, 0.0 us)
Async XLA Ops:
  6.5 77.8 %copy-start = (bf16[512,3072]{1,0:T(8,128)(2,1)S(1)}, bf16[512,3072]{1,0:T(8,128)(2,1)}, u32[]{:S(2)}) copy-start(bf16[512,3072]{1,0:T(8,128)(2,1)} %param.3) | copy-start | bytes 9437188
  6.5 317.4 %reduce-scatter.2.cloned.1.call-start = ((), (), s32[]{:S(2)}) async-start(), calls=%async_computation.1 | async-start | bytes 9584640 | tf_op jit(solution)/shard_map/reduce_scatter | solution.py:58
  6.5 70.2 %collective-permute-start = (bf16[512,3072]{1,0:T(8,128)(2,1)}, bf16[512,3072]{1,0:T(8,128)(2,1)}, u32[]{:S(2)}, u32[]{:S(2)}) collective-permute-start(bf16[512,3072]{1,0:T(8,128)(2,1)} %param.3), channel_id=1, source_target_pairs={{0,1},{1,2},{2,3},{3,0},{4,5},{5,6},{6,7},{7,4},{8,9},{9,10},{10,1... | collective-permute-start | bytes 9437192 | tf_op jit(solution)/shard_map/ppermute | solution.py:21
  8.0 82.2 %collective-permute-start.1 = (bf16[512,3072]{1,0:T(8,128)(2,1)}, bf16[512,3072]{1,0:T(8,128)(2,1)}, u32[]{:S(2)}, u32[]{:S(2)}) collective-permute-start(bf16[512,3072]{1,0:T(8,128)(2,1)} %param.3), channel_id=1, source_target_pairs={{0,3},{1,0},{2,1},{3,2},{4,7},{5,4},{6,5},{7,6},{8,11},{9,8},{10,9... | collective-permute-start | bytes 9437192 | tf_op jit(solution)/shard_map/ppermute | solution.py:26
  76.7 69.0 %collective-permute-start.2 = (bf16[512,3072]{1,0:T(8,128)(2,1)}, bf16[512,3072]{1,0:T(8,128)(2,1)}, u32[]{:S(2)}, u32[]{:S(2)}) collective-permute-start(bf16[512,3072]{1,0:T(8,128)(2,1)} %collective-permute-done), channel_id=1, source_target_pairs={{0,1},{1,2},{2,3},{3,0},{4,5},{5,6},{6,7},{7,4},{8,9},{9,10},{10,1... | collective-permute-start | bytes 9437192 | tf_op jit(solution)/shard_map/ppermute | solution.py:21
  84.4 65.1 %copy-start.1 = (bf16[2048,768]{1,0:T(8,128)(2,1)S(1)}, bf16[2048,768]{1,0:T(8,128)(2,1)}, u32[]{:S(2)}) copy-start(bf16[2048,768]{1,0:T(8,128)(2,1)} %param.2) | copy-start | bytes 9437188
  149.4 15.5 %copy-start.2 = (bf16[2048,768]{1,0:T(8,128)(2,1)S(1)}, bf16[2048,768]{1,0:T(8,128)(2,1)}, u32[]{:S(2)}) copy-start(bf16[2048,768]{1,0:T(8,128)(2,1)} %param.2) | copy-start | bytes 9437188
Sparse Core Ops, SparseCore 0:
  165.0 158.8 reduce-scatter.1
